TPU v7x, 32 devices: a whole 2x2x4 slice. The times are simulated.
32 devices in a mesh: row: 8 (over y, x, core), col: 4 (over z).
Axes of the slice: x: 2, y: 2, z: 4, core: 2. Of those that a mesh axis runs over, the one named last changes fastest.
Arguments:
- tiles: float32 [8, 4, 4, 512, 512], P('row', 'col'), may hold values from 0 to 16777212, as said below
- tile_index: int32 [8, 4, 4, 2], P('row', 'col'), may hold values from 0 to 3, as said below
- tile_count: int32 [8, 4], P('row', 'col'), may hold values from 0 to 4, as said below
- iterate: float32 [8192, 32], P(('row', 'col')), may hold values from 0 to 16777212, as said below
- basis: float32 [8192, 32], P(('row', 'col')), may hold values from 0 to 16777212, as said below
- coefficients: float32 [256, 32, 32], P(('row', 'col')), may hold values from 0 to 16777212, as said below
- start_degree: int32 [1], replicated, may hold values from 1 to 255
Outputs:
- scaled_iterate: float32 [8192, 32], P(('row', 'col'))
Inputs may be any that keep to these rules, and one draw needn't show every extreme that they name: `tiles`: integers 0 to 16777212. `iterate`: integers 0 to 16777212. `basis`: integers 0 to 16777212. `coefficients`: integers 0 to 16777212. tile_index[..., 0] lies in 0 to 1 and tile_index[..., 1] in 0 to 3; the 4 slots of one device name distinct tiles, unoccupied slots included; unoccupied slots hold arbitrary entries. `tile_count`: some device has 4 occupied slots.
All inputs are finite; a program needn't handle non-finite values.
Results may differ from a plain program's by a relative error of at most 0.0003.
Values sent between devices are 32-bit elements; how exact they have to be, the bound alone decides.
A program may use at most 64 MiB of HBM per device.

v0:
```python
import jax
import jax.numpy as jnp
from jax import lax
from jax.sharding import PartitionSpec as P

STEPS = 2
PRIME = 16777213
RADIX = 16777216


def from_root(block, axis, source):
    block = jnp.where(lax.axis_index(axis) == source, block, jnp.zeros_like(block))
    return lax.psum(block, axis)


def fold_word(value):
    value = value % RADIX + 3 * (value // RADIX)
    return jnp.where(value >= PRIME, value - PRIME, value)


def add_mod(first, second):
    total = first + second
    return jnp.where(total >= PRIME, total - PRIME, total)


def shift_mod(value, shift):
    while shift > 0:
        amount = min(shift, 7)
        value = fold_word(value * 2**amount)
        shift = shift - amount
    return value


def split_limbs(values, bits, count):
    whole = values.astype(jnp.int32)
    return [(whole // 2 ** (bits * place) % 2**bits).astype(jnp.bfloat16) for place in range(count)]


def combine_limbs(product, left_bits, right_bits, width):
    whole = product.astype(jnp.int32)
    total = None
    for left in range(whole.shape[-3]):
        for right in range(whole.shape[-1] // width):
            piece = whole[..., left, :, right * width : (right + 1) * width]
            term = shift_mod(piece, left_bits * left + right_bits * right)
            total = term if total is None else add_mod(total, term)
    return total


def tile_products(tile_limbs, gathered, column_slots, tile):
    column_limbs = jnp.concatenate(split_limbs(gathered, 6, 4), axis=1)
    windows = jax.vmap(
        lambda column: lax.dynamic_slice_in_dim(column_limbs, column * tile, tile, 0)
    )(column_slots)
    product = jnp.einsum("tlik,tkc->tlic", tile_limbs, windows, preferred_element_type=jnp.float32)
    return combine_limbs(product, 8, 6, gathered.shape[1])


def on_device(tiles, tile_index, tile_count, iterate, basis, coefficients, start_degree):
    block = tiles[0, 0]
    tile = block.shape[-1]
    slots = block.shape[0]
    rows_dev = iterate.shape[0]
    width = iterate.shape[1]
    count_col = lax.axis_size("col")
    block_rows = rows_dev * count_col // tile
    per_device = coefficients.shape[0]
    tile_limbs = jnp.stack(split_limbs(block, 8, 3), axis=1)
    row_slots = tile_index[0, 0, :, 0]
    column_slots = tile_index[0, 0, :, 1]
    used = jnp.arange(slots) < tile_count[0, 0]
    match = row_slots[:, None] == jnp.arange(block_rows)[None, :]
    basis_limbs = jnp.stack(split_limbs(basis, 8, 3))
    degree = start_degree[0]
    current = iterate
    for step in range(STEPS):
        wanted = degree - step
        holding = lax.dynamic_index_in_dim(coefficients, wanted % per_device, 0, keepdims=False)
        coef = from_root(holding, ("row", "col"), wanted // per_device)
        packed = lax.all_gather(current.reshape(-1, 128), "row", axis=0, tiled=True)
        gathered = packed.reshape(-1, width)
        residues = tile_products(tile_limbs, gathered, column_slots, tile)
        kept = jnp.where(used[:, None, None], residues, 0)
        partial_value = (
            jnp.sum(jnp.where(match[:, :, None, None], kept[:, None], 0), axis=0) % PRIME
        )
        partial_value = partial_value.reshape(block_rows * tile, width)
        pieces = partial_value.astype(jnp.float32).reshape(count_col, -1, 128)
        arrived = lax.all_to_all(pieces, "col", split_axis=0, concat_axis=0, tiled=True)
        local = (jnp.sum(arrived.astype(jnp.int32), axis=0) % PRIME).reshape(rows_dev, width)
        coef_limbs = jnp.concatenate(split_limbs(coef, 8, 3), axis=1)
        basis_product = jnp.einsum(
            "lrk,kc->lrc", basis_limbs, coef_limbs, preferred_element_type=jnp.float32
        )
        basis_term = combine_limbs(basis_product, 8, 8, width)
        current = add_mod(local, basis_term).astype(jnp.float32)
    return current / PRIME


def solution(mesh):
    in_specs = (
        P("row", "col", None, None, None),
        P("row", "col", None, None),
        P("row", "col"),
        P(("row", "col"), None),
        P(("row", "col"), None),
        P(("row", "col"), None, None),
        P(),
    )
    out_specs = P(("row", "col"), None)
    return jax.shard_map(
        on_device, mesh=mesh, in_specs=in_specs, out_specs=out_specs, check_vma=False
    )
```

profile of v0, /device:TPU:0, one launch (start us, length us, event | category | flops | bytes accessed | tf_op | source)
XLA Modules:
  0.0 145.7 jit_solution(8975279407004597319)
XLA Ops:
  1.4 11.8 %fusion = (bf16[4,1,512,512]{3,2,1,0:T(8,128)(2,1)S(1)}, bf16[4,1,512,512]{3,2,1,0:T(8,128)(2,1)}, bf16[4,1,512,512]{3,2,1,0:T(8,128)(2,1)}) fusion(f32[1,1,4,512,512]{4,3,2,1,0:T(8,128)} %param.7), kind=kLoop, calls=%fused_computation.19 | loop fusion | flops 57671680 | bytes 10485760 | tf_op jit(solution)/shard_map/convert_element_type | solution.py:36
  13.3 11.0 %all_gather.6 = f32[512,128]{1,0:T(8,128)S(1)} all-gather(f32[64,128]{1,0:T(8,128)S(1)} %reshape.310), channel_id=1, replica_groups=mesh['row'=8,'col'=4] {'row'}, dimensions={0}, use_global_device_ids=true | all-gather | bytes 294912 | tf_op jit(solution)/shard_map/all_gather | solution.py:80
  24.6 3.1 %fusion.13 = (bf16[2048,32]{1,0:T(8,128)(2,1)S(1)}, bf16[2048,32]{1,0:T(8,128)(2,1)S(1)}, bf16[2048,32]{1,0:T(8,128)(2,1)S(1)}, bf16[2048,32]{1,0:T(8,128)(2,1)S(1)}) fusion(s32[2048,32]{1,0:T(8,128)S(1)} %convert_element_type.162), kind=kLoop, calls=%fused_computation.76 | loop fusion | flops 4980736 | bytes 786432 | tf_op jit(solution)/shard_map/convert_element_type | solution.py:36
  28.4 5.7 %while.2 = (s32[]{:T(128)}, bf16[2048,128]{1,0:T(8,128)(2,1)S(1)}, s32[4,2]{0,1:T(2,128)S(1)}, bf16[4,512,128]{2,1,0:T(8,128)(2,1)S(1)}, s32[]{:T(128)}) while((s32[]{:T(128)}, bf16[2048,128]{1,0:T(8,128)(2,1)S(1)}, s32[4,2]{0,1:T(2,128)S(1)}, bf16[4,512,128]{2,1,0:T(8,128)(2,1)S(1)}, s32[]{:T(128)}) %tuple.53), condition=%wide.while_cond, body=%wide.while_body.sunk | while | flops 2 | bytes 262249 | solution.py:53
  29.1 0.7 bitcast_dynamic-update-slice_fusion.4
  30.6 0.7 bitcast_dynamic-update-slice_fusion.4
  32.0 0.7 bitcast_dynamic-update-slice_fusion.4
  33.4 0.7 bitcast_dynamic-update-slice_fusion.4
  34.9 3.9 %fusion.11 = s32[4,3,512,128]{2,3,1,0:T(8,128)S(1)} fusion(bf16[4,1,512,512]{3,2,1,0:T(8,128)(2,1)} %get-tuple-element.40, bf16[4,1,512,512]{3,2,1,0:T(8,128)(2,1)} %get-tuple-element.41, bf16[4,1,512,512]{3,2,1,0:T(8,128)(2,1)S(1)} %get-tuple-element.39, bf16[4,512,128]{2,1,0:T(8,128)(2,1)S(1)} %get-tuple-element.12), kind=kOutput, calls=%fused_computation.32 | convolution fusion | flops 812384256 | bytes 9961472 | tf_op jit(solution)/shard_map/tlik,tkc->tlic/dot_general | solution.py:55
  38.9 9.4 %fusion.205 = s32[4,512,32]{1,2,0:T(8,128)S(1)} fusion(s32[4,3,512,128]{2,3,1,0:T(8,128)S(1)} %fusion.11, pred[4]{0:T(512)(128)(4,1)S(1)} %iota_compare_fusion.1), kind=kLoop, calls=%fused_computation.692 | loop fusion | flops 57016320 | bytes 3407876 | tf_op jit(solution)/shard_map/jit(_where)/broadcast_in_dim | solution.py:85
  49.5 4.9 %all-to-all-start = ((f32[4,64,128]{2,1,0:T(8,128)}), f32[4,64,128]{2,1,0:T(8,128)S(1)}, u32[]{:S(2)}, u32[]{:S(2)}) async-start(f32[4,64,128]{2,1,0:T(8,128)} %fusion.505), calls=%async_computation | async-start | bytes 262144 | tf_op jit(solution)/shard_map/all_to_all | solution.py:89
  56.0 40.0 %all-reduce.1 = (f32[32,32]{1,0:T(8,128)S(1)}, f32[32,32]{1,0:T(8,128)S(1)}) all-reduce(f32[32,32]{1,0:T(8,128)S(1)} %get-tuple-element.60, f32[32,32]{1,0:T(8,128)S(1)} %get-tuple-element.59), channel_id=1, replica_groups=mesh['row'=8,'col'=4] {'row','col'}, use_global_device_ids=true, to_apply=%region_2.3 | all-reduce | flops 2048 | bytes 16384 | tf_op jit(solution)/shard_map/psum | solution.py:13
  98.2 1.0 fusion.645
  99.2 10.3 %all_gather.7 = f32[512,128]{1,0:T(8,128)S(1)} all-gather(f32[64,128]{1,0:T(8,128)S(1)} %fusion.645), channel_id=1, replica_groups=mesh['row'=8,'col'=4] {'row'}, dimensions={0}, use_global_device_ids=true | all-gather | bytes 294912 | tf_op jit(solution)/shard_map/all_gather | solution.py:80
  109.8 3.1 %fusion.22 = (bf16[2048,32]{1,0:T(8,128)(2,1)S(1)}, bf16[2048,32]{1,0:T(8,128)(2,1)S(1)}, bf16[2048,32]{1,0:T(8,128)(2,1)S(1)}, bf16[2048,32]{1,0:T(8,128)(2,1)S(1)}) fusion(s32[2048,32]{1,0:T(8,128)S(1)} %convert_element_type.181), kind=kLoop, calls=%fused_computation.85 | loop fusion | flops 4980736 | bytes 786432 | tf_op jit(solution)/shard_map/convert_element_type | solution.py:36
  113.6 5.7 %while.3 = (s32[]{:T(128)}, bf16[2048,128]{1,0:T(8,128)(2,1)S(1)}, s32[4,2]{0,1:T(2,128)S(1)}, bf16[4,512,128]{2,1,0:T(8,128)(2,1)S(1)}, s32[]{:T(128)}) while((s32[]{:T(128)}, bf16[2048,128]{1,0:T(8,128)(2,1)S(1)}, s32[4,2]{0,1:T(2,128)S(1)}, bf16[4,512,128]{2,1,0:T(8,128)(2,1)S(1)}, s32[]{:T(128)}) %tuple.59), condition=%wide.while_cond.1, body=%wide.while_body.1.sunk | while | flops 2 | bytes 262249 | solution.py:53
  114.3 0.7 bitcast_dynamic-update-slice_fusion.5
  115.7 0.7 bitcast_dynamic-update-slice_fusion.5
  117.2 0.7 bitcast_dynamic-update-slice_fusion.5
  119.4 3.9 %fusion.12 = s32[4,3,512,128]{2,3,1,0:T(8,128)S(1)} fusion(bf16[4,1,512,512]{3,2,1,0:T(8,128)(2,1)} %get-tuple-element.40, bf16[4,1,512,512]{3,2,1,0:T(8,128)(2,1)} %get-tuple-element.41, bf16[4,1,512,512]{3,2,1,0:T(8,128)(2,1)S(1)} %get-tuple-element.39, bf16[4,512,128]{2,1,0:T(8,128)(2,1)S(1)} %get-tuple-element.20), kind=kOutput, calls=%fused_computation.33 | convolution fusion | flops 812384256 | bytes 9961472 | tf_op jit(solution)/shard_map/tlik,tkc->tlic/dot_general | solution.py:55
  123.3 9.4 %fusion.240 = s32[4,512,32]{1,2,0:T(8,128)S(1)} fusion(s32[4,3,512,128]{2,3,1,0:T(8,128)S(1)} %fusion.12, pred[4]{0:T(512)(128)(4,1)S(1)} %iota_compare_fusion.1), kind=kLoop, calls=%fused_computation.727 | loop fusion | flops 57016320 | bytes 3407876 | tf_op jit(solution)/shard_map/jit(_where)/broadcast_in_dim | solution.py:85
  134.0 3.5 %all-to-all-start.1 = ((f32[4,64,128]{2,1,0:T(8,128)}), f32[4,64,128]{2,1,0:T(8,128)S(1)}, u32[]{:S(2)}, u32[]{:S(2)}) async-start(f32[4,64,128]{2,1,0:T(8,128)} %fusion.506), calls=%async_computation.1 | async-start | bytes 262144 | tf_op jit(solution)/shard_map/all_to_all | solution.py:89
  137.8 6.1 %all-to-all-done.1 = f32[4,64,128]{2,1,0:T(8,128)S(1)} async-done(((f32[4,64,128]{2,1,0:T(8,128)}), f32[4,64,128]{2,1,0:T(8,128)S(1)}, u32[]{:S(2)}, u32[]{:S(2)}) %all-to-all-start.1) | async-done | bytes 131104 | tf_op jit(solution)/shard_map/all_to_all | solution.py:89
  144.1 1.6 %fusion.673 = f32[256,32]{0,1:T(8,128)} fusion(s32[256,32]{0,1:T(8,128)S(1)} %copy.44, s32[3,256,96]{1,2,0:T(8,128)S(1)} %convolution_convert_fusion), kind=kLoop, calls=%fused_computation.1601 | loop fusion | flops 5677056 | bytes 360448 | tf_op jit(solution)/shard_map/div | solution.py:97
  (76 shorter events, 15.7 us)
Async XLA Ops:
  1.4 11.8 %copy-start = (f32[256,32]{0,1:T(8,128)S(1)}, f32[256,32]{0,1:T(8,128)}, u32[]{:S(2)}) copy-start(f32[256,32]{0,1:T(8,128)} %param.10) | copy-start | bytes 98308
  38.8 16.2 %copy-start.1 = (f32[256,32]{0,1:T(8,128)S(1)}, f32[256,32]{0,1:T(8,128)}, u32[]{:S(2)}) copy-start(f32[256,32]{0,1:T(8,128)} %param.11) | copy-start | bytes 98308
  49.5 48.7 %all-to-all-start = ((f32[4,64,128]{2,1,0:T(8,128)}), f32[4,64,128]{2,1,0:T(8,128)S(1)}, u32[]{:S(2)}, u32[]{:S(2)}) async-start(f32[4,64,128]{2,1,0:T(8,128)} %fusion.505), calls=%async_computation | async-start | bytes 262144 | tf_op jit(solution)/shard_map/all_to_all | solution.py:89
  134.0 10.0 %all-to-all-start.1 = ((f32[4,64,128]{2,1,0:T(8,128)}), f32[4,64,128]{2,1,0:T(8,128)S(1)}, u32[]{:S(2)}, u32[]{:S(2)}) async-start(f32[4,64,128]{2,1,0:T(8,128)} %fusion.506), calls=%async_computation.1 | async-start | bytes 262144 | tf_op jit(solution)/shard_map/all_to_all | solution.py:89
where the time goes:
time: 146 us
  blocking collectives  61.2 us (42%)
  other arithmetic  44.1 us (30%)
  local copies, waits for them, and re-layouts  15.4 us (11%)
  matrix products  8.49 us (6%)
  starting transfers between devices  8.42 us (6%)
  waiting for transfers between devices  6.1 us (4%)
  between operations  1.76 us (1%)
    psum x1, blocking collectives, from_root(): return lax.psum(block, axis)  40 us
    all_gather x2, blocking collectives, on_device(): packed = lax.all_gather(current.reshape(-1, 128), 'row', axis=0, tiled=True)  21.3 us
    broadcast_in_dim x2, other arithmetic, on_device(): jnp.where(match[:, :, None, None], kept[:, None], 0)  18.8 us
    convert_element_type x4, other arithmetic, split_limbs(): (whole // 2 ** (bits * place) % 2 ** bits).astype(jnp.bfloat16)  18 us
    gather x24, local copies, waits for them, and re-layouts  11.3 us
    all_to_all x2, starting transfers between devices, on_device(): lax.all_to_all(pieces, 'col', split_axis=0, concat_axis=0, tiled=True)  8.42 us
    dot_general x2, matrix products, tile_products(): jnp.einsum('tlik,tkc->tlic', tile_limbs, windows, preferred_element_type=...  7.85 us
    all_to_all x2, waiting for transfers between devices, on_device(): lax.all_to_all(pieces, 'col', split_axis=0, concat_axis=0, tiled=True)  6.1 us
  transfers between devices with their start and end apart: 2, of which 1 were waited for; matrix products, arithmetic and copies ran while one was open for 2% of the time, Pallas kernels for 0%

commit v1 on v0

--- a/solution.py
+++ b/solution.py
@@ -10,7 +10,7 @@
 
 def from_root(block, axis, source):
     block = jnp.where(lax.axis_index(axis) == source, block, jnp.zeros_like(block))
-    return lax.psum(block, axis)
+    return jnp.sum(lax.all_gather(block, axis), axis=0)
 
 
 def fold_word(value):

time: 146 us -> 244 us (1.67)
  blocking collectives: 61.2 us -> 160 us
    all_gather x0 -> x2, blocking collectives: none -> 140 us  [from_root(): return jnp.sum(lax.all_gather(block, axis), axis=0)]
    psum x1 -> x0, blocking collectives: 40 us -> none  [from_root(): return lax.psum(block, axis)]
    convert_element_type x4 -> x5, other arithmetic: 18 us -> 18 us  [split_limbs(): (whole // 2 ** (bits * place) % 2 ** bits).astype(jnp.bfloat16)]
  transfers between devices with their start and end apart: 2 -> 2, of which waited for: 1 -> 1; matrix products, arithmetic and copies ran while one was open for 2% -> 1% of each run, Pallas kernels for 0% -> 0%
where the time goes in v1:
time: 244 us; the launch traced here: 243 us
  blocking collectives  160 us (66%)
  other arithmetic  44.3 us (18%)
  local copies, waits for them, and re-layouts  14.3 us (6%)
  matrix products  8.49 us (3%)
  starting transfers between devices  8.19 us (3%)
  waiting for transfers between devices  6.1 us (2%)
    all_gather x2, blocking collectives, from_root(): return jnp.sum(lax.all_gather(block, axis), axis=0)  140 us
    all_gather x2, blocking collectives, on_device(): packed = lax.all_gather(current.reshape(-1, 128), 'row', axis=0, tiled=True)  20.5 us
    broadcast_in_dim x2, other arithmetic, on_device(): jnp.where(match[:, :, None, None], kept[:, None], 0)  18.8 us
    convert_element_type x5, other arithmetic, split_limbs(): (whole // 2 ** (bits * place) % 2 ** bits).astype(jnp.bfloat16)  18 us
    gather x24, local copies, waits for them, and re-layouts  10.2 us
    all_to_all x2, starting transfers between devices, on_device(): lax.all_to_all(pieces, 'col', split_axis=0, concat_axis=0, tiled=True)  8.19 us
    dot_general x2, matrix products, tile_products(): jnp.einsum('tlik,tkc->tlic', tile_limbs, windows, preferred_element_type=...  7.85 us
    all_to_all x2, waiting for transfers between devices, on_device(): lax.all_to_all(pieces, 'col', split_axis=0, concat_axis=0, tiled=True)  6.1 us
  transfers between devices with their start and end apart: 2, of which 1 were waited for; matrix products, arithmetic and copies ran while one was open for 1% of the time, Pallas kernels for 0%

profile of v1, /device:TPU:0, one launch (start us, length us, event | category | flops | bytes accessed | tf_op | source)
XLA Modules:
  0.0 243.3 jit_solution(3327664039528326349)
XLA Ops:
  0.0 0.7 compare_select_fusion.158
  0.7 0.7 slice_bitcast_fusion.1
  1.4 11.8 %fusion = (bf16[4,1,512,512]{3,2,1,0:T(8,128)(2,1)S(1)}, bf16[4,1,512,512]{3,2,1,0:T(8,128)(2,1)}, bf16[4,1,512,512]{3,2,1,0:T(8,128)(2,1)}) fusion(f32[1,1,4,512,512]{4,3,2,1,0:T(8,128)} %param.7), kind=kLoop, calls=%fused_computation.19 | loop fusion | flops 57671680 | bytes 10485760 | tf_op jit(solution)/shard_map/convert_element_type | solution.py:36
  13.3 11.0 %all_gather.14 = f32[512,128]{1,0:T(8,128)S(1)} all-gather(f32[64,128]{1,0:T(8,128)S(1)} %reshape.304), channel_id=1, replica_groups=mesh['row'=8,'col'=4] {'row'}, dimensions={0}, use_global_device_ids=true | all-gather | bytes 294912 | tf_op jit(solution)/shard_map/all_gather | solution.py:80
  24.6 3.1 %fusion.13 = (bf16[2048,32]{1,0:T(8,128)(2,1)S(1)}, bf16[2048,32]{1,0:T(8,128)(2,1)S(1)}, bf16[2048,32]{1,0:T(8,128)(2,1)S(1)}, bf16[2048,32]{1,0:T(8,128)(2,1)S(1)}) fusion(s32[2048,32]{1,0:T(8,128)S(1)} %convert_element_type.162), kind=kLoop, calls=%fused_computation.76 | loop fusion | flops 4980736 | bytes 786432 | tf_op jit(solution)/shard_map/convert_element_type | solution.py:36
  27.7 0.7 pad_maximum_fusion.7
  28.5 5.2 %while.2 = (s32[]{:T(128)}, bf16[2048,128]{1,0:T(8,128)(2,1)S(1)}, s32[4,2]{0,1:T(2,128)S(1)}, bf16[4,512,128]{2,1,0:T(8,128)(2,1)S(1)}, s32[]{:T(128)}) while((s32[]{:T(128)}, bf16[2048,128]{1,0:T(8,128)(2,1)S(1)}, s32[4,2]{0,1:T(2,128)S(1)}, bf16[4,512,128]{2,1,0:T(8,128)(2,1)S(1)}, s32[]{:T(128)}) %tuple.50), condition=%wide.while_cond, body=%wide.while_body.sunk | while | flops 2 | bytes 262249 | solution.py:53
  29.1 0.7 bitcast_dynamic-update-slice_fusion.4
  34.4 3.9 %fusion.11 = s32[4,3,512,128]{2,3,1,0:T(8,128)S(1)} fusion(bf16[4,1,512,512]{3,2,1,0:T(8,128)(2,1)} %get-tuple-element.38, bf16[4,1,512,512]{3,2,1,0:T(8,128)(2,1)} %get-tuple-element.39, bf16[4,1,512,512]{3,2,1,0:T(8,128)(2,1)S(1)} %get-tuple-element.37, bf16[4,512,128]{2,1,0:T(8,128)(2,1)S(1)} %get-tuple-element.12), kind=kOutput, calls=%fused_computation.32 | convolution fusion | flops 812384256 | bytes 9961472 | tf_op jit(solution)/shard_map/tlik,tkc->tlic/dot_general | solution.py:55
  38.3 9.4 %fusion.205 = s32[4,512,32]{1,2,0:T(8,128)S(1)} fusion(s32[4,3,512,128]{2,3,1,0:T(8,128)S(1)} %fusion.11, pred[4]{0:T(512)(128)(4,1)S(1)} %iota_compare_fusion.1), kind=kLoop, calls=%fused_computation.692 | loop fusion | flops 57016320 | bytes 3407876 | tf_op jit(solution)/shard_map/jit(_where)/broadcast_in_dim | solution.py:85
  49.0 4.9 %all-to-all-start = ((f32[4,64,128]{2,1,0:T(8,128)}), f32[4,64,128]{2,1,0:T(8,128)S(1)}, u32[]{:S(2)}, u32[]{:S(2)}) async-start(f32[4,64,128]{2,1,0:T(8,128)} %fusion.505), calls=%async_computation | async-start | bytes 262144 | tf_op jit(solution)/shard_map/all_to_all | solution.py:89
  54.7 0.7 dynamic-slice_select_fusion
  55.4 71.7 %all_gather.15 = f32[32,32,32]{2,1,0:T(8,128)S(1)} all-gather(f32[1,32,32]{2,1,0:T(8,128)S(1)} %get-tuple-element.58), channel_id=1, replica_groups=mesh['row'=8,'col'=4] {'row','col'}, dimensions={0}, use_global_device_ids=true | all-gather | bytes 135168 | tf_op jit(solution)/shard_map/all_gather | solution.py:13
  129.4 67.8 %all_gather.17 = f32[32,32,32]{2,1,0:T(8,128)S(1)} all-gather(f32[1,32,32]{2,1,0:T(8,128)S(1)} %get-tuple-element.57), channel_id=1, replica_groups=mesh['row'=8,'col'=4] {'row','col'}, dimensions={0}, use_global_device_ids=true | all-gather | bytes 135168 | tf_op jit(solution)/shard_map/all_gather | solution.py:13
  197.3 1.0 fusion.645
  198.3 9.5 %all_gather.16 = f32[512,128]{1,0:T(8,128)S(1)} all-gather(f32[64,128]{1,0:T(8,128)S(1)} %fusion.645), channel_id=1, replica_groups=mesh['row'=8,'col'=4] {'row'}, dimensions={0}, use_global_device_ids=true | all-gather | bytes 294912 | tf_op jit(solution)/shard_map/all_gather | solution.py:80
  208.1 3.1 %fusion.22 = (bf16[2048,32]{1,0:T(8,128)(2,1)S(1)}, bf16[2048,32]{1,0:T(8,128)(2,1)S(1)}, bf16[2048,32]{1,0:T(8,128)(2,1)S(1)}, bf16[2048,32]{1,0:T(8,128)(2,1)S(1)}) fusion(s32[2048,32]{1,0:T(8,128)S(1)} %convert_element_type.181), kind=kLoop, calls=%fused_computation.85 | loop fusion | flops 4980736 | bytes 786432 | tf_op jit(solution)/shard_map/convert_element_type | solution.py:36
  211.1 0.7 pad_maximum_fusion.8
  211.9 5.2 %while.3 = (s32[]{:T(128)}, bf16[2048,128]{1,0:T(8,128)(2,1)S(1)}, s32[4,2]{0,1:T(2,128)S(1)}, bf16[4,512,128]{2,1,0:T(8,128)(2,1)S(1)}, s32[]{:T(128)}) while((s32[]{:T(128)}, bf16[2048,128]{1,0:T(8,128)(2,1)S(1)}, s32[4,2]{0,1:T(2,128)S(1)}, bf16[4,512,128]{2,1,0:T(8,128)(2,1)S(1)}, s32[]{:T(128)}) %tuple.56), condition=%wide.while_cond.1, body=%wide.while_body.1.sunk | while | flops 2 | bytes 262249 | solution.py:53
  217.1 3.9 %fusion.12 = s32[4,3,512,128]{2,3,1,0:T(8,128)S(1)} fusion(bf16[4,1,512,512]{3,2,1,0:T(8,128)(2,1)} %get-tuple-element.38, bf16[4,1,512,512]{3,2,1,0:T(8,128)(2,1)} %get-tuple-element.39, bf16[4,1,512,512]{3,2,1,0:T(8,128)(2,1)S(1)} %get-tuple-element.37, bf16[4,512,128]{2,1,0:T(8,128)(2,1)S(1)} %get-tuple-element.20), kind=kOutput, calls=%fused_computation.33 | convolution fusion | flops 812384256 | bytes 9961472 | tf_op jit(solution)/shard_map/tlik,tkc->tlic/dot_general | solution.py:55
  221.0 9.4 %fusion.240 = s32[4,512,32]{1,2,0:T(8,128)S(1)} fusion(s32[4,3,512,128]{2,3,1,0:T(8,128)S(1)} %fusion.12, pred[4]{0:T(512)(128)(4,1)S(1)} %iota_compare_fusion.1), kind=kLoop, calls=%fused_computation.727 | loop fusion | flops 57016320 | bytes 3407876 | tf_op jit(solution)/shard_map/jit(_where)/broadcast_in_dim | solution.py:85
  231.7 3.3 %all-to-all-start.1 = ((f32[4,64,128]{2,1,0:T(8,128)}), f32[4,64,128]{2,1,0:T(8,128)S(1)}, u32[]{:S(2)}, u32[]{:S(2)}) async-start(f32[4,64,128]{2,1,0:T(8,128)} %fusion.506), calls=%async_computation.1 | async-start | bytes 262144 | tf_op jit(solution)/shard_map/all_to_all | solution.py:89
  235.4 6.1 %all-to-all-done.1 = f32[4,64,128]{2,1,0:T(8,128)S(1)} async-done(((f32[4,64,128]{2,1,0:T(8,128)}), f32[4,64,128]{2,1,0:T(8,128)S(1)}, u32[]{:S(2)}, u32[]{:S(2)}) %all-to-all-start.1) | async-done | bytes 131104 | tf_op jit(solution)/shard_map/all_to_all | solution.py:89
  241.7 1.6 fusion.673
  (80 shorter events, 15.7 us)
Async XLA Ops:
  1.4 11.8 %copy-start = (f32[256,32]{0,1:T(8,128)S(1)}, f32[256,32]{0,1:T(8,128)}, u32[]{:S(2)}) copy-start(f32[256,32]{0,1:T(8,128)} %param.10) | copy-start | bytes 98308
  38.3 16.2 %copy-start.1 = (f32[256,32]{0,1:T(8,128)S(1)}, f32[256,32]{0,1:T(8,128)}, u32[]{:S(2)}) copy-start(f32[256,32]{0,1:T(8,128)} %param.11) | copy-start | bytes 98308
  49.0 148.3 %all-to-all-start = ((f32[4,64,128]{2,1,0:T(8,128)}), f32[4,64,128]{2,1,0:T(8,128)S(1)}, u32[]{:S(2)}, u32[]{:S(2)}) async-start(f32[4,64,128]{2,1,0:T(8,128)} %fusion.505), calls=%async_computation | async-start | bytes 262144 | tf_op jit(solution)/shard_map/all_to_all | solution.py:89
  231.7 9.8 %all-to-all-start.1 = ((f32[4,64,128]{2,1,0:T(8,128)}), f32[4,64,128]{2,1,0:T(8,128)S(1)}, u32[]{:S(2)}, u32[]{:S(2)}) async-start(f32[4,64,128]{2,1,0:T(8,128)} %fusion.506), calls=%async_computation.1 | async-start | bytes 262144 | tf_op jit(solution)/shard_map/all_to_all | solution.py:89
